TPU v7x, 256 devices: a whole 4x4x8 slice. The times are simulated.
256 devices in a mesh: row: 16 (over y, x), col: 16 (over z, core).
Axes of the slice: x: 4, y: 4, z: 8, core: 2. Of those that a mesh axis runs over, the one named last changes fastest.
Arguments:
- trail: float32 [2, 16, 512, 2, 16, 512], P(None, 'row', None, None, 'col'), may hold values from -6 to 6
- panel: float32 [2, 16, 512, 512], P(None, 'row', None, 'col'), may hold values from -6 to 6
- row_basis: float32 [2, 16, 64, 512], P(None, 'row', None, 'col'), may hold values from -0.75 to 0.75
- row_coeff: float32 [2, 16, 64, 512], P(None, 'row', None, 'col'), may hold values from -0.25 to 0.25
- col_basis: float32 [2, 16, 64, 512], P(None, 'col', None, 'row'), may hold values from -0.75 to 0.75
- col_scaled: float32 [2, 16, 64, 512], P(None, 'col', None, 'row'), may hold values from -0.25 to 0.25
- pivot_basis: float32 [64, 512], P(None, 'col'), may hold values from -0.75 to 0.75
- pivot_scaled: float32 [64, 512], replicated, may hold values from -0.25 to 0.25
- sketch: float32 [64, 512], replicated, may hold values from -6 to 6
- perm: int32 [512], replicated, may hold values from 0 to 511, each once
- pair_kind: int32 [256], replicated, may hold values from 0 to 1
- pivot_values: float32 [3, 256], replicated, may hold values from -3 to 3, as said below
Outputs:
- trail_out: float32 [2, 16, 512, 2, 16, 512], P(None, 'row', None, None, 'col')
- basis_out: float32 [2, 16, 64, 512], P(None, 'row')
- coeff_out: float32 [2, 16, 64, 512], P(None, 'row')
Inputs may be any that keep to these rules, and one draw needn't show every extreme that they name: `pivot_values`: rows 0 and 1 have magnitudes between 0.5 and 0.7; row 2 has magnitude 1.2 or more.
All inputs are finite; a program needn't handle non-finite values.
Results may differ from a plain program's by a relative error of at most 0.00013.
Values sent between devices are 32-bit elements; how exact they have to be, the bound alone decides.
A program may use at most 64 MiB of HBM per device.

v0:
```python
import jax
import jax.numpy as jnp
from jax import lax
from jax.sharding import PartitionSpec as P


def gather_turned(arrays, axis, dims):
    turned = [jnp.moveaxis(a, dim, 0) for a, dim in zip(arrays, dims)]
    both = jnp.concatenate([t.reshape(len(t), -1) for t in turned], axis=1)
    filled, at, outs = (lax.all_gather(both, axis, axis=0, tiled=True), 0, [])
    for t, dim in zip(turned, dims):
        share = filled[:, at : at + t[0].size].reshape(-1, *t.shape[1:])
        outs.append(jnp.moveaxis(share, 0, dim))
        at += t[0].size
    return tuple(outs)


def total_of_pieces(array, axis):
    return lax.all_gather(array, axis).sum(0)


def pair_apply(rows, pair_kind, pivot_values):
    shaped = rows.reshape(rows.shape[:-1] + (rows.shape[-1] // 2, 2))
    first_in = shaped[..., 0]
    second_in = shaped[..., 1]
    diag_one = pivot_values[0]
    diag_two = pivot_values[1]
    offdiag = pivot_values[2]
    determinant = diag_one * diag_two - offdiag * offdiag
    twin = pair_kind == 1
    first = jnp.where(
        twin, (first_in * diag_two - second_in * offdiag) / determinant, first_in / diag_one
    )
    second = jnp.where(
        twin, (second_in * diag_one - first_in * offdiag) / determinant, second_in / diag_two
    )
    return jnp.stack([first, second], axis=-1).reshape(rows.shape)


def tri_solve(lower, rhs):
    return jax.vmap(lambda low, right: jax.scipy.linalg.solve_triangular(low, right, lower=True))(
        lower, rhs
    )


def body(
    trail,
    panel,
    row_basis,
    row_coeff,
    col_basis,
    col_scaled,
    pivot_basis,
    pivot_scaled,
    sketch,
    perm,
    pair_kind,
    pivot_values,
):
    highest = lax.Precision.HIGHEST
    width = sketch.shape[1]
    block = panel.shape[3]
    xrows, yrows = gather_turned((row_basis, row_coeff), "col", (3, 3))
    zcols, gcols = gather_turned((col_basis, col_scaled), "row", (3, 3))
    xrows = xrows[:, 0]
    yrows = yrows[:, 0]
    zcols = zcols[:, 0]
    gcols = gcols[:, 0]
    core = jnp.einsum("arp,bsp->arbs", yrows, gcols, precision=highest)
    left = jnp.einsum("arp,arbs->apbs", xrows, core, precision=highest)
    change = jnp.einsum("apbs,bsq->apbq", left, zcols, precision=highest)
    trail_out = trail - change[:, None, :, :, None, :]
    pcore = jnp.einsum("arp,sp->ars", yrows, pivot_scaled, precision=highest)
    pleft = jnp.einsum("arp,ars->aps", xrows, pcore, precision=highest)
    updated = panel[:, 0] - jnp.einsum("aps,sq->apq", pleft, pivot_basis, precision=highest)
    scaled_t = pair_apply(sketch, pair_kind, pivot_values)
    column_ids = lax.axis_index("col") * block + jnp.arange(block, dtype=jnp.int32)
    selector = (perm[:, None] == column_ids[None, :]).astype(jnp.float32)
    local_sketch = jnp.dot(scaled_t, selector, precision=highest)
    partial_range = jnp.einsum("apq,rq->arp", updated, local_sketch, precision=highest)
    range_t = total_of_pieces(partial_range, "col")
    gram = jnp.einsum("arp,asp->ars", range_t, range_t, precision=highest) / width
    basis = tri_solve(jnp.linalg.cholesky(gram), range_t)
    projected_part = jnp.einsum("arp,apq->arq", basis, updated, precision=highest)
    projected = lax.all_gather(projected_part, "col", axis=2, tiled=True)
    permuted = jnp.take(projected, perm, axis=2)
    coeff = pair_apply(permuted, pair_kind, pivot_values) / jnp.sqrt(jnp.float32(width))
    return (trail_out, basis[:, None], coeff[:, None])


def solution(mesh):
    return jax.shard_map(
        body,
        mesh=mesh,
        in_specs=(
            P(None, "row", None, None, "col", None),
            P(None, "row", None, "col"),
            P(None, "row", None, "col"),
            P(None, "row", None, "col"),
            P(None, "col", None, "row"),
            P(None, "col", None, "row"),
            P(None, "col"),
            P(),
            P(),
            P(),
            P(),
            P(),
        ),
        out_specs=(
            P(None, "row", None, None, "col", None),
            P(None, "row", None, None),
            P(None, "row", None, None),
        ),
        check_vma=False,
    )
```

profile of v0, /device:TPU:1, one launch (start us, length us, event | category | flops | bytes accessed | tf_op | source)
XLA Modules:
  0.0 150.3 jit_solution(10058551639044590301)
XLA Ops:
  7.3 0.8 broadcast_compare_fusion
  8.0 0.8 fusion.11
  8.8 0.8 copy.78
  9.7 0.8 copy.79
  10.6 1.0 copy.85
  11.6 22.7 %all_gather.16 = f32[512,256]{1,0:T(8,128)S(1)} all-gather(f32[32,256]{1,0:T(8,128)S(1)} %pad_maximum_fusion.2), channel_id=1, replica_groups=mesh['row'=16,'col'=16] {'col'}, dimensions={0}, use_global_device_ids=true | all-gather | bytes 557056 | tf_op jit(solution)/shard_map/all_gather | solution.py:10
  34.7 2.2 %broadcast_select_fusion.3 = (f32[64,256,1]{0,2,1:T(1,128)S(1)}, f32[64,256,1]{0,2,1:T(1,128)S(1)}) fusion(pred[256]{0:T(512)(128)(4,1)S(1)} %broadcast_compare_fusion, f32[64,256,2]{0,2,1:T(2,128)S(1)} %bitcast.108, f32[256]{0:T(256)S(1)} %bitcast.120, f32[256]{0:T(256)S(1)} %bitcast.126, f32[256]{0:T(256)S(1)} %bitcast.123, f32[256]{0:T(256)S(1)} %bitcast.117), kind=kLoop, calls=%fused_computation.11 | loop fusion | flops 196608 | bytes 266496 | tf_op jit(solution)/shard_map/jit(_where)/select_n | solution.py:31
  37.2 0.5 fusion.1
  38.8 1.1 convolution_bitcast_fusion
  40.4 19.9 %all_gather.15 = f32[512,256]{1,0:T(8,128)S(1)} all-gather(f32[32,256]{1,0:T(8,128)S(1)} %pad_maximum_fusion.1), channel_id=1, replica_groups=mesh['row'=16,'col'=16] {'row'}, dimensions={0}, use_global_device_ids=true | all-gather | bytes 557056 | tf_op jit(solution)/shard_map/all_gather | solution.py:10
  60.6 11.0 %copy.84 = f32[2,1,512,2,1,512]{2,5,0,3,4,1:T(8,128)} copy(f32[2,1,512,2,1,512]{5,4,3,2,1,0:T(1,128)} %param.12) | data formatting | bytes 8388608 | tf_op args[0]
  71.6 0.5 fusion.12
  72.1 0.6 fusion.13
  72.7 6.7 %bitcast_subtract_fusion = f32[2,1,512,2,1,512]{2,5,0,3,4,1:T(8,128)} fusion(f32[2,1,512,2,1,512]{2,5,0,3,4,1:T(8,128)} %copy.84, f32[2,64,512,1]{2,1,3,0:T(8,128)S(1)} %bitcast.109, f32[2,512,2,64]{1,3,0,2:T(8,128)S(1)} %fusion.13), kind=kOutput, calls=%fused_computation.1 | convolution fusion | flops 806354944 | bytes 9175040 | tf_op jit(solution)/shard_map/apbs,bsq->apbq/dot_general | solution.py:71
  79.4 10.9 %copy.91 = f32[2,1,512,2,1,512]{5,4,3,2,1,0:T(1,128)} copy(f32[2,1,512,2,1,512]{2,5,0,3,4,1:T(8,128)} %bitcast_subtract_fusion) | data formatting | bytes 8388608
  90.3 2.6 %reduce_sum.9 = f32[2,64,512]{2,1,0:T(8,128)S(1)} reduce(f32[16,2,64,512]{3,2,1,0:T(8,128)} %bitcast.101, f32[]{:T(128)} %constant.67.clone.1), dimensions={0}, to_apply=%region_0.1 | reduce | flops 983040 | bytes 4456452 | tf_op jit(solution)/shard_map/reduce_sum | solution.py:19
  93.5 11.7 %custom-call.8 = f32[2,64,64]{2,1,0:T(8,128)S(1)} custom-call(f32[2,64,64]{2,1,0:T(8,128)S(1)} %fusion.7), custom_call_target="Cholesky" | custom-call | tf_op jit(solution)/shard_map/jit(cholesky)/cholesky | solution.py:83
  105.4 9.8 %custom-call.9 = f32[2,1,64,64]{2,3,1,0:T(8,128)S(1)} custom-call(f32[2,1,64,64]{3,2,1,0:T(8,128)S(1)} %select_bitcast_fusion), custom_call_target="InvertDiagBlocksLowerTriangular" | custom-call | tf_op jit(solution)/shard_map/vmap(jit(_solve_triangular))/triangular_solve | solution.py:41
  116.1 20.6 %all_gather.19 = f32[2,64,512]{1,2,0:T(8,128)S(1)} all-gather(f32[2,64,32]{1,2,0:T(8,128)S(1)} %fusion.16), channel_id=1, replica_groups=mesh['row'=16,'col'=16] {'col'}, dimensions={2}, use_global_device_ids=true | all-gather | bytes 278528 | tf_op jit(solution)/shard_map/all_gather | solution.py:85
  137.0 2.1 %gather_fusion = f32[512,2,64]{2,1,0:T(2,128)S(1)} fusion(f32[2,64,512]{1,0,2:T(2,128)S(1)} %copy.89, s32[1024]{0:T(1024)S(1)} %pad_clamp_fusion), kind=kCustom, calls=%fused_computation | custom fusion | bytes 526336 | tf_op jit(solution)/shard_map/jit(_take)/gather | solution.py:86
  139.1 0.6 copy_select_fusion
  139.8 2.2 %broadcast_select_fusion.1 = (f32[2,64,256,1]{1,3,2,0:T(1,128)S(1)}, f32[2,64,256,1]{1,3,2,0:T(1,128)S(1)}) fusion(pred[256]{0:T(512)(128)(4,1)S(1)} %broadcast_compare_fusion, f32[2,64,256,2]{1,3,2,0:T(2,128)S(1)} %copy_select_fusion, f32[256]{0:T(256)S(1)} %bitcast.122, f32[256]{0:T(256)S(1)} %multiply_subtract_fusion, f32[256]{0:T(256)S(1)} %bitcast.125, ...), kind=kLoop, calls=%fused_computation.8 | loop fusion | flops 393216 | bytes 528640 | tf_op jit(solution)/shard_map/jit(_where)/select_n | solution.py:31
  142.0 0.6 maximum_multiply_fusion
  142.6 0.9 copy.93
  (52 shorter events, 4.6 us)
Async XLA Ops:
  7.2 30.0 %copy-start = (f32[64,512]{1,0:T(8,128)S(1)}, f32[64,512]{1,0:T(8,128)}, u32[]{:S(2)}) copy-start(f32[64,512]{1,0:T(8,128)} %param.19) | copy-start | bytes 393220
  7.2 30.9 %copy-start.5 = (s32[512]{0:T(512)S(1)}, s32[512]{0:T(512)}, u32[]{:S(2)}) copy-start(s32[512]{0:T(512)} %param.21) | copy-start | bytes 6148
  7.2 31.3 %copy-start.6 = (f32[64,32]{0,1:T(8,128)S(1)}, f32[64,32]{0,1:T(8,128)}, u32[]{:S(2)}) copy-start(f32[64,32]{0,1:T(8,128)} %param.18) | copy-start | bytes 24580
  7.2 31.3 %copy-start.2 = (f32[2,1,512,32]{2,3,1,0:T(8,128)S(1)}, f32[2,1,512,32]{2,3,1,0:T(8,128)}, u32[]{:S(2)}) copy-start(f32[2,1,512,32]{2,3,1,0:T(8,128)} %param.13) | copy-start | bytes 393220
  7.2 33.0 %copy-start.3 = (f32[2,1,64,32]{2,3,1,0:T(8,128)S(1)}, f32[2,1,64,32]{2,3,1,0:T(8,128)}, u32[]{:S(2)}) copy-start(f32[2,1,64,32]{2,3,1,0:T(8,128)} %param.16) | copy-start | bytes 49156
  7.2 33.1 %copy-start.4 = (f32[2,1,64,32]{2,3,1,0:T(8,128)S(1)}, f32[2,1,64,32]{2,3,1,0:T(8,128)}, u32[]{:S(2)}) copy-start(f32[2,1,64,32]{2,3,1,0:T(8,128)} %param.17) | copy-start | bytes 49156
  7.2 83.1 %all-gather.3.cloned.1.call-start = ((), (), s32[]{:S(2)}) async-start(), calls=%async_computation | async-start | bytes 4456448 | tf_op jit(solution)/shard_map/all_gather | solution.py:19
  115.7 27.8 %copy-start.1 = (f32[2,64,512]{2,1,0:T(8,128)}, f32[2,64,512]{2,1,0:T(8,128)S(1)}, u32[]{:S(2)}) copy-start(f32[2,64,512]{2,1,0:T(8,128)S(1)} %fusion.5) | copy-start | bytes 786436
Sparse Core Ops, SparseCore 0:
  40.1 40.0 all-gather.2
where the time goes:
time: 151 us; the launch traced here: 150 us
  blocking collectives  63.2 us (42%)
  other arithmetic  32 us (21%)
  local copies, waits for them, and re-layouts  29.1 us (19%)
  between operations  14.4 us (10%)
  matrix products  11.7 us (8%)
    all_gather x2, blocking collectives, gather_turned(): filled, at, outs = (lax.all_gather(both, axis, axis=0, tiled=True), 0, [])  42.6 us
    unnamed x18, local copies, waits for them, and re-layouts  23.8 us
    all_gather x1, blocking collectives, body(): projected = lax.all_gather(projected_part, 'col', axis=2, tiled=True)  20.6 us
    another operation x4, other arithmetic, body(): basis = tri_solve(jnp.linalg.cholesky(gram), range_t)  11.9 us
    another operation x3, other arithmetic, tri_solve(): jax.scipy.linalg.solve_triangular(low, right, lower=True)  9.92 us
    dot_general x1, matrix products, body(): change = jnp.einsum('apbs,bsq->apbq', left, zcols, precision=highest)  6.7 us
    select_n x2, other arithmetic, pair_apply(): jnp.where(twin, (first_in * diag_two - second_in * offdiag) / determinant...  4.37 us
  transfers between devices with their start and end apart: 1, of which 0 were waited for; matrix products, arithmetic and copies ran while one was open for 20% of the time, Pallas kernels for 0%

commit v1 on v0

--- a/solution.py
+++ b/solution.py
@@ -1,7 +1,49 @@
+import functools
 import jax
 import jax.numpy as jnp
 from jax import lax
 from jax.sharding import PartitionSpec as P
+
+
+def panels_note(z, row_axis, row_dim):
+    val = lax.axis_size(row_axis)
+    all_rows = lax.axis_index(row_axis)
+    arr_next, passed, reached = (val, all_rows, z.shape[row_dim])
+    tmp = lax.dynamic_update_slice_in_dim(
+        jnp.zeros(
+            tuple(
+                (
+                    tick * arr_next if src_i == row_dim else tick
+                    for src_i, tick in enumerate(z.shape)
+                )
+            ),
+            z.dtype,
+        ),
+        z,
+        passed * reached,
+        axis=row_dim,
+    )
+    built = piece_next = z
+    for ii in range(1, arr_next // 2 + 1):
+        built = lax.ppermute(
+            built, row_axis, tuple(((src_i, (src_i + 1) % arr_next) for src_i in range(arr_next)))
+        )
+        tmp = lax.dynamic_update_slice_in_dim(
+            tmp, built, (passed - ii) % arr_next * reached, axis=row_dim
+        )
+        if 2 * ii < arr_next:
+            piece_next = lax.ppermute(
+                piece_next,
+                row_axis,
+                tuple(((src_i, (src_i - 1) % arr_next) for src_i in range(arr_next))),
+            )
+            tmp = lax.dynamic_update_slice_in_dim(
+                tmp, piece_next, (passed + ii) % arr_next * reached, axis=row_dim
+            )
+    return tmp
+
+
+region_rest = functools.partial(panels_note, row_axis="col", row_dim=2)
 
 
 def gather_turned(arrays, axis, dims):
@@ -82,7 +124,7 @@
     gram = jnp.einsum("arp,asp->ars", range_t, range_t, precision=highest) / width
     basis = tri_solve(jnp.linalg.cholesky(gram), range_t)
     projected_part = jnp.einsum("arp,apq->arq", basis, updated, precision=highest)
-    projected = lax.all_gather(projected_part, "col", axis=2, tiled=True)
+    projected = region_rest(projected_part)
     permuted = jnp.take(projected, perm, axis=2)
     coeff = pair_apply(permuted, pair_kind, pivot_values) / jnp.sqrt(jnp.float32(width))
     return (trail_out, basis[:, None], coeff[:, None])

time: 151 us -> 170 us (1.13); the launches traced: 150 us -> 167 us
  starting transfers between devices: 0.04 us -> 23.9 us
  blocking collectives: 63.2 us -> 42.8 us
  waiting for transfers between devices: 0.04 us -> 13 us
    ppermute x0 -> x15, starting transfers between devices: none -> 23.8 us  [the longest x7 21.5 us: panels_note(): lax.ppermute(piece_next, row_axis, tuple(((src_i, (src_i - 1) % arr_next)...]
    all_gather x1 -> x0, blocking collectives: 20.6 us -> none  [body(): projected = lax.all_gather(projected_part, 'col', axis=2, tiled=True)]
    ppermute x0 -> x15, waiting for transfers between devices: none -> 12.9 us  [the longest x8 8.07 us: panels_note(): lax.ppermute(built, row_axis, tuple(((src_i, (src_i + 1) % arr_next) for...]
  transfers between devices with their start and end apart: 1 -> 16, of which waited for: 0 -> 8; matrix products, arithmetic and copies ran while one was open for 20% -> 19% of each run, Pallas kernels for 0% -> 0%
where the time goes in v1:
time: 170 us; the launch traced here: 167 us
  blocking collectives  42.8 us (25%)
  other arithmetic  31.7 us (19%)
  local copies, waits for them, and re-layouts  29.5 us (17%)
  starting transfers between devices  23.9 us (14%)
  between operations  14.7 us (9%)
  waiting for transfers between devices  13 us (8%)
  matrix products  11.6 us (7%)
    all_gather x2, blocking collectives, gather_turned(): filled, at, outs = (lax.all_gather(both, axis, axis=0, tiled=True), 0, [])  42.8 us
    unnamed x18, local copies, waits for them, and re-layouts  23.8 us
    ppermute x7, starting transfers between devices, panels_note(): lax.ppermute(piece_next, row_axis, tuple(((src_i, (src_i - 1) % arr_next)...  21.5 us
    another operation x4, other arithmetic, body(): basis = tri_solve(jnp.linalg.cholesky(gram), range_t)  11.9 us
    another operation x3, other arithmetic, tri_solve(): jax.scipy.linalg.solve_triangular(low, right, lower=True)  9.92 us
    ppermute x8, waiting for transfers between devices, panels_note(): lax.ppermute(built, row_axis, tuple(((src_i, (src_i + 1) % arr_next) for...  8.07 us
    dot_general x1, matrix products, body(): change = jnp.einsum('apbs,bsq->apbq', left, zcols, precision=highest)  6.69 us
    ppermute x7, waiting for transfers between devices, panels_note(): lax.ppermute(piece_next, row_axis, tuple(((src_i, (src_i - 1) % arr_next)...  4.85 us
  transfers between devices with their start and end apart: 16, of which 8 were waited for; matrix products, arithmetic and copies ran while one was open for 19% of the time, Pallas kernels for 0%

profile of v1, /device:TPU:1, one launch (start us, length us, event | category | flops | bytes accessed | tf_op | source)
XLA Modules:
  0.0 167.1 jit_solution(7907485998177092797)
XLA Ops:
  10.6 1.0 copy.129
  11.6 22.7 %all_gather.13 = f32[512,256]{1,0:T(8,128)S(1)} all-gather(f32[32,256]{1,0:T(8,128)S(1)} %pad_maximum_fusion.2), channel_id=1, replica_groups=mesh['row'=16,'col'=16] {'col'}, dimensions={0}, use_global_device_ids=true | all-gather | bytes 557056 | tf_op jit(solution)/shard_map/all_gather | solution.py:52
  34.7 2.2 %broadcast_select_fusion.4 = (f32[64,256,1]{0,2,1:T(1,128)S(1)}, f32[64,256,1]{0,2,1:T(1,128)S(1)}) fusion(pred[256]{0:T(512)(128)(4,1)S(1)} %broadcast_compare_fusion, f32[64,256,2]{0,2,1:T(2,128)S(1)} %bitcast.108, f32[256]{0:T(256)S(1)} %bitcast.120, f32[256]{0:T(256)S(1)} %bitcast.126, f32[256]{0:T(256)S(1)} %bitcast.123, f32[256]{0:T(256)S(1)} %bitcast.117), kind=kLoop, calls=%fused_computation.11 | loop fusion | flops 196608 | bytes 266496 | tf_op jit(solution)/shard_map/jit(_where)/select_n | solution.py:73
  38.8 1.1 convolution_bitcast_fusion
  40.7 20.0 %all_gather.12 = f32[512,256]{1,0:T(8,128)S(1)} all-gather(f32[32,256]{1,0:T(8,128)S(1)} %pad_maximum_fusion.1), channel_id=1, replica_groups=mesh['row'=16,'col'=16] {'row'}, dimensions={0}, use_global_device_ids=true | all-gather | bytes 557056 | tf_op jit(solution)/shard_map/all_gather | solution.py:52
  61.1 11.0 %copy.128 = f32[2,1,512,2,1,512]{2,5,0,3,4,1:T(8,128)} copy(f32[2,1,512,2,1,512]{5,4,3,2,1,0:T(1,128)} %param.12) | data formatting | bytes 8388608 | tf_op args[0]
  73.1 6.7 %bitcast_subtract_fusion = f32[2,1,512,2,1,512]{2,5,0,3,4,1:T(8,128)} fusion(f32[2,1,512,2,1,512]{2,5,0,3,4,1:T(8,128)} %copy.128, f32[2,64,512,1]{2,1,3,0:T(8,128)S(1)} %bitcast.109, f32[2,512,2,64]{1,3,0,2:T(8,128)S(1)} %fusion.13), kind=kOutput, calls=%fused_computation.1 | convolution fusion | flops 806354944 | bytes 9175040 | tf_op jit(solution)/shard_map/apbs,bsq->apbq/dot_general | solution.py:113
  79.8 10.9 %copy.150 = f32[2,1,512,2,1,512]{5,4,3,2,1,0:T(1,128)} copy(f32[2,1,512,2,1,512]{2,5,0,3,4,1:T(8,128)} %bitcast_subtract_fusion) | data formatting | bytes 8388608
  90.8 2.6 %reduce_sum.9 = f32[2,64,512]{2,1,0:T(8,128)S(1)} reduce(f32[16,2,64,512]{3,2,1,0:T(8,128)} %bitcast.100, f32[]{:T(128)} %constant.152.clone.1), dimensions={0}, to_apply=%region_0.1 | reduce | flops 983040 | bytes 4456452 | tf_op jit(solution)/shard_map/reduce_sum | solution.py:61
  93.9 11.7 %custom-call.8 = f32[2,64,64]{2,1,0:T(8,128)S(1)} custom-call(f32[2,64,64]{2,1,0:T(8,128)S(1)} %fusion.7), custom_call_target="Cholesky" | custom-call | tf_op jit(solution)/shard_map/jit(cholesky)/cholesky | solution.py:125
  105.9 9.8 %custom-call.9 = f32[2,1,64,64]{2,3,1,0:T(8,128)S(1)} custom-call(f32[2,1,64,64]{3,2,1,0:T(8,128)S(1)} %select_bitcast_fusion), custom_call_target="InvertDiagBlocksLowerTriangular" | custom-call | tf_op jit(solution)/shard_map/vmap(jit(_solve_triangular))/triangular_solve | solution.py:83
  116.5 4.9 %collective-permute-start.1 = (f32[2,64,32]{1,2,0:T(8,128)S(1)}, f32[2,64,32]{1,2,0:T(8,128)S(1)}, u32[]{:S(2)}, u32[]{:S(2)}) collective-permute-start(f32[2,64,32]{1,2,0:T(8,128)S(1)} %fusion.16), channel_id=1, source_target_pairs={{0,15},{1,0},{2,1},{3,2},{4,3},{5,4},{6,5},{7,6},{8,7},{9,8},{10,9... | collective-permute-start | bytes 49160 | tf_op jit(solution)/shard_map/ppermute | solution.py:35
  123.0 1.7 %collective-permute-start.2 = (f32[2,64,32]{1,2,0:T(8,128)S(1)}, f32[2,64,32]{1,2,0:T(8,128)S(1)}, u32[]{:S(2)}, u32[]{:S(2)}) collective-permute-start(f32[2,64,32]{1,2,0:T(8,128)S(1)} %collective-permute-done), channel_id=1, source_target_pairs={{0,1},{1,2},{2,3},{3,4},{4,5},{5,6},{6,7},{7,8},{8,9},{9,10},{10,1... | collective-permute-start | bytes 49160 | tf_op jit(solution)/shard_map/ppermute | solution.py:28
  124.8 0.9 collective-permute-done.3
  125.7 1.9 %collective-permute-start.5 = (f32[2,64,32]{1,2,0:T(8,128)S(1)}, f32[2,64,32]{1,2,0:T(8,128)S(1)}, u32[]{:S(2)}, u32[]{:S(2)}) collective-permute-start(f32[2,64,32]{1,2,0:T(8,128)S(1)} %collective-permute-done.3), channel_id=1, source_target_pairs={{0,15},{1,0},{2,1},{3,2},{4,3},{5,4},{6,5},{7,6},{8,7},{9,8},{10,9... | collective-permute-start | bytes 49160 | tf_op jit(solution)/shard_map/ppermute | solution.py:35
  129.0 3.1 %collective-permute-start.7 = (f32[2,64,32]{1,2,0:T(8,128)S(1)}, f32[2,64,32]{1,2,0:T(8,128)S(1)}, u32[]{:S(2)}, u32[]{:S(2)}) collective-permute-start(f32[2,64,32]{1,2,0:T(8,128)S(1)} %collective-permute-done.5), channel_id=1, source_target_pairs={{0,15},{1,0},{2,1},{3,2},{4,3},{5,4},{6,5},{7,6},{8,7},{9,8},{10,9... | collective-permute-start | bytes 49160 | tf_op jit(solution)/shard_map/ppermute | solution.py:35
  133.0 3.7 %collective-permute-start.9 = (f32[2,64,32]{1,2,0:T(8,128)S(1)}, f32[2,64,32]{1,2,0:T(8,128)S(1)}, u32[]{:S(2)}, u32[]{:S(2)}) collective-permute-start(f32[2,64,32]{1,2,0:T(8,128)S(1)} %collective-permute-done.7), channel_id=1, source_target_pairs={{0,15},{1,0},{2,1},{3,2},{4,3},{5,4},{6,5},{7,6},{8,7},{9,8},{10,9... | collective-permute-start | bytes 49160 | tf_op jit(solution)/shard_map/ppermute | solution.py:35
  137.5 3.7 %collective-permute-start.11 = (f32[2,64,32]{1,2,0:T(8,128)S(1)}, f32[2,64,32]{1,2,0:T(8,128)S(1)}, u32[]{:S(2)}, u32[]{:S(2)}) collective-permute-start(f32[2,64,32]{1,2,0:T(8,128)S(1)} %collective-permute-done.9), channel_id=1, source_target_pairs={{0,15},{1,0},{2,1},{3,2},{4,3},{5,4},{6,5},{7,6},{8,7},{9,8},{10,9... | collective-permute-start | bytes 49160 | tf_op jit(solution)/shard_map/ppermute | solution.py:35
  142.1 3.7 %collective-permute-start.13 = (f32[2,64,32]{1,2,0:T(8,128)S(1)}, f32[2,64,32]{1,2,0:T(8,128)S(1)}, u32[]{:S(2)}, u32[]{:S(2)}) collective-permute-start(f32[2,64,32]{1,2,0:T(8,128)S(1)} %collective-permute-done.11), channel_id=1, source_target_pairs={{0,15},{1,0},{2,1},{3,2},{4,3},{5,4},{6,5},{7,6},{8,7},{9,8},{10,9... | collective-permute-start | bytes 49160 | tf_op jit(solution)/shard_map/ppermute | solution.py:35
  145.9 3.6 %collective-permute-done.12 = f32[2,64,32]{1,2,0:T(8,128)S(1)} collective-permute-done((f32[2,64,32]{1,2,0:T(8,128)S(1)}, f32[2,64,32]{1,2,0:T(8,128)S(1)}, u32[]{:S(2)}, u32[]{:S(2)}) %collective-permute-start.12) | collective-permute-done | bytes 16416 | tf_op jit(solution)/shard_map/ppermute | solution.py:28
  149.5 4.5 %collective-permute-done.14 = f32[2,64,32]{1,2,0:T(8,128)S(1)} collective-permute-done((f32[2,64,32]{1,2,0:T(8,128)S(1)}, f32[2,64,32]{1,2,0:T(8,128)S(1)}, u32[]{:S(2)}, u32[]{:S(2)}) %collective-permute-start.14) | collective-permute-done | bytes 16416 | tf_op jit(solution)/shard_map/ppermute | solution.py:28
  154.0 2.1 %gather_fusion = f32[512,2,64]{2,1,0:T(2,128)S(1)} fusion(f32[2,64,512]{1,0,2:T(2,128)S(1)} %copy_dynamic-update-slice_fusion, s32[1024]{0:T(1024)S(1)} %pad_clamp_fusion), kind=kCustom, calls=%fused_computation | custom fusion | bytes 526336 | tf_op jit(solution)/shard_map/jit(_take)/gather | solution.py:128
  156.5 2.2 %broadcast_select_fusion.1 = (f32[2,64,256,1]{1,3,2,0:T(1,128)S(1)}, f32[2,64,256,1]{1,3,2,0:T(1,128)S(1)}) fusion(pred[256]{0:T(512)(128)(4,1)S(1)} %broadcast_compare_fusion, f32[2,64,256,2]{1,3,2,0:T(2,128)S(1)} %broadcast_select_fusion.2, f32[256]{0:T(256)S(1)} %bitcast.122, f32[256]{0:T(256)S(1)} %multiply_subtract_fusion, f32[256]{0:T(256)S(1)} %bitcast.125, ...), kind=kLoop, calls=%fused_computation.7 | loop fusion | flops 393216 | bytes 528640 | tf_op jit(solution)/shard_map/jit(_where)/select_n | solution.py:73
  159.4 0.9 copy.152
  (98 shorter events, 15.9 us)
Async XLA Ops:
  7.2 30.0 %copy-start = (f32[64,512]{1,0:T(8,128)S(1)}, f32[64,512]{1,0:T(8,128)}, u32[]{:S(2)}) copy-start(f32[64,512]{1,0:T(8,128)} %param.19) | copy-start | bytes 393220
  7.2 30.9 %copy-start.5 = (s32[512]{0:T(512)S(1)}, s32[512]{0:T(512)}, u32[]{:S(2)}) copy-start(s32[512]{0:T(512)} %param.21) | copy-start | bytes 6148
  7.2 31.3 %copy-start.6 = (f32[64,32]{0,1:T(8,128)S(1)}, f32[64,32]{0,1:T(8,128)}, u32[]{:S(2)}) copy-start(f32[64,32]{0,1:T(8,128)} %param.18) | copy-start | bytes 24580
  7.2 31.3 %copy-start.2 = (f32[2,1,512,32]{2,3,1,0:T(8,128)S(1)}, f32[2,1,512,32]{2,3,1,0:T(8,128)}, u32[]{:S(2)}) copy-start(f32[2,1,512,32]{2,3,1,0:T(8,128)} %param.13) | copy-start | bytes 393220
  7.2 33.2 %copy-start.3 = (f32[2,1,64,32]{2,3,1,0:T(8,128)S(1)}, f32[2,1,64,32]{2,3,1,0:T(8,128)}, u32[]{:S(2)}) copy-start(f32[2,1,64,32]{2,3,1,0:T(8,128)} %param.16) | copy-start | bytes 49156
  7.2 33.4 %copy-start.4 = (f32[2,1,64,32]{2,3,1,0:T(8,128)S(1)}, f32[2,1,64,32]{2,3,1,0:T(8,128)}, u32[]{:S(2)}) copy-start(f32[2,1,64,32]{2,3,1,0:T(8,128)} %param.17) | copy-start | bytes 49156
  7.2 83.6 %all-gather.3.cloned.1.call-start = ((), (), s32[]{:S(2)}) async-start(), calls=%async_computation | async-start | bytes 4456448 | tf_op jit(solution)/shard_map/all_gather | solution.py:61
  116.1 44.1 %copy-start.1 = (f32[2,64,512]{2,1,0:T(8,128)}, f32[2,64,512]{2,1,0:T(8,128)S(1)}, u32[]{:S(2)}) copy-start(f32[2,64,512]{2,1,0:T(8,128)S(1)} %fusion.5) | copy-start | bytes 786436
  116.5 5.9 %collective-permute-start.1 = (f32[2,64,32]{1,2,0:T(8,128)S(1)}, f32[2,64,32]{1,2,0:T(8,128)S(1)}, u32[]{:S(2)}, u32[]{:S(2)}) collective-permute-start(f32[2,64,32]{1,2,0:T(8,128)S(1)} %fusion.16), channel_id=1, source_target_pairs={{0,15},{1,0},{2,1},{3,2},{4,3},{5,4},{6,5},{7,6},{8,7},{9,8},{10,9... | collective-permute-start | bytes 49160 | tf_op jit(solution)/shard_map/ppermute | solution.py:35
  121.4 1.6 collective-permute-start
  122.4 3.3 %collective-permute-start.3 = (f32[2,64,32]{1,2,0:T(8,128)S(1)}, f32[2,64,32]{1,2,0:T(8,128)S(1)}, u32[]{:S(2)}, u32[]{:S(2)}) collective-permute-start(f32[2,64,32]{1,2,0:T(8,128)S(1)} %collective-permute-done.1), channel_id=1, source_target_pairs={{0,15},{1,0},{2,1},{3,2},{4,3},{5,4},{6,5},{7,6},{8,7},{9,8},{10,9... | collective-permute-start | bytes 49160 | tf_op jit(solution)/shard_map/ppermute | solution.py:35
  123.0 4.6 %collective-permute-start.2 = (f32[2,64,32]{1,2,0:T(8,128)S(1)}, f32[2,64,32]{1,2,0:T(8,128)S(1)}, u32[]{:S(2)}, u32[]{:S(2)}) collective-permute-start(f32[2,64,32]{1,2,0:T(8,128)S(1)} %collective-permute-done), channel_id=1, source_target_pairs={{0,1},{1,2},{2,3},{3,4},{4,5},{5,6},{6,7},{7,8},{8,9},{9,10},{10,1... | collective-permute-start | bytes 49160 | tf_op jit(solution)/shard_map/ppermute | solution.py:28
  125.7 3.3 %collective-permute-start.5 = (f32[2,64,32]{1,2,0:T(8,128)S(1)}, f32[2,64,32]{1,2,0:T(8,128)S(1)}, u32[]{:S(2)}, u32[]{:S(2)}) collective-permute-start(f32[2,64,32]{1,2,0:T(8,128)S(1)} %collective-permute-done.3), channel_id=1, source_target_pairs={{0,15},{1,0},{2,1},{3,2},{4,3},{5,4},{6,5},{7,6},{8,7},{9,8},{10,9... | collective-permute-start | bytes 49160 | tf_op jit(solution)/shard_map/ppermute | solution.py:35
  127.6 4.6 %collective-permute-start.4 = (f32[2,64,32]{1,2,0:T(8,128)S(1)}, f32[2,64,32]{1,2,0:T(8,128)S(1)}, u32[]{:S(2)}, u32[]{:S(2)}) collective-permute-start(f32[2,64,32]{1,2,0:T(8,128)S(1)} %collective-permute-done.2), channel_id=1, source_target_pairs={{0,1},{1,2},{2,3},{3,4},{4,5},{5,6},{6,7},{7,8},{8,9},{9,10},{10,1... | collective-permute-start | bytes 49160 | tf_op jit(solution)/shard_map/ppermute | solution.py:28
  129.0 3.9 %collective-permute-start.7 = (f32[2,64,32]{1,2,0:T(8,128)S(1)}, f32[2,64,32]{1,2,0:T(8,128)S(1)}, u32[]{:S(2)}, u32[]{:S(2)}) collective-permute-start(f32[2,64,32]{1,2,0:T(8,128)S(1)} %collective-permute-done.5), channel_id=1, source_target_pairs={{0,15},{1,0},{2,1},{3,2},{4,3},{5,4},{6,5},{7,6},{8,7},{9,8},{10,9... | collective-permute-start | bytes 49160 | tf_op jit(solution)/shard_map/ppermute | solution.py:35
  132.1 4.6 %collective-permute-start.6 = (f32[2,64,32]{1,2,0:T(8,128)S(1)}, f32[2,64,32]{1,2,0:T(8,128)S(1)}, u32[]{:S(2)}, u32[]{:S(2)}) collective-permute-start(f32[2,64,32]{1,2,0:T(8,128)S(1)} %collective-permute-done.4), channel_id=1, source_target_pairs={{0,1},{1,2},{2,3},{3,4},{4,5},{5,6},{6,7},{7,8},{8,9},{9,10},{10,1... | collective-permute-start | bytes 49160 | tf_op jit(solution)/shard_map/ppermute | solution.py:28
  133.0 4.6 %collective-permute-start.9 = (f32[2,64,32]{1,2,0:T(8,128)S(1)}, f32[2,64,32]{1,2,0:T(8,128)S(1)}, u32[]{:S(2)}, u32[]{:S(2)}) collective-permute-start(f32[2,64,32]{1,2,0:T(8,128)S(1)} %collective-permute-done.7), channel_id=1, source_target_pairs={{0,15},{1,0},{2,1},{3,2},{4,3},{5,4},{6,5},{7,6},{8,7},{9,8},{10,9... | collective-permute-start | bytes 49160 | tf_op jit(solution)/shard_map/ppermute | solution.py:35
  136.7 4.6 %collective-permute-start.8 = (f32[2,64,32]{1,2,0:T(8,128)S(1)}, f32[2,64,32]{1,2,0:T(8,128)S(1)}, u32[]{:S(2)}, u32[]{:S(2)}) collective-permute-start(f32[2,64,32]{1,2,0:T(8,128)S(1)} %collective-permute-done.6), channel_id=1, source_target_pairs={{0,1},{1,2},{2,3},{3,4},{4,5},{5,6},{6,7},{7,8},{8,9},{9,10},{10,1... | collective-permute-start | bytes 49160 | tf_op jit(solution)/shard_map/ppermute | solution.py:28
  137.5 4.6 %collective-permute-start.11 = (f32[2,64,32]{1,2,0:T(8,128)S(1)}, f32[2,64,32]{1,2,0:T(8,128)S(1)}, u32[]{:S(2)}, u32[]{:S(2)}) collective-permute-start(f32[2,64,32]{1,2,0:T(8,128)S(1)} %collective-permute-done.9), channel_id=1, source_target_pairs={{0,15},{1,0},{2,1},{3,2},{4,3},{5,4},{6,5},{7,6},{8,7},{9,8},{10,9... | collective-permute-start | bytes 49160 | tf_op jit(solution)/shard_map/ppermute | solution.py:35
  141.2 4.6 %collective-permute-start.10 = (f32[2,64,32]{1,2,0:T(8,128)S(1)}, f32[2,64,32]{1,2,0:T(8,128)S(1)}, u32[]{:S(2)}, u32[]{:S(2)}) collective-permute-start(f32[2,64,32]{1,2,0:T(8,128)S(1)} %collective-permute-done.8), channel_id=1, source_target_pairs={{0,1},{1,2},{2,3},{3,4},{4,5},{5,6},{6,7},{7,8},{8,9},{9,10},{10,1... | collective-permute-start | bytes 49160 | tf_op jit(solution)/shard_map/ppermute | solution.py:28
  142.1 7.4 %collective-permute-start.13 = (f32[2,64,32]{1,2,0:T(8,128)S(1)}, f32[2,64,32]{1,2,0:T(8,128)S(1)}, u32[]{:S(2)}, u32[]{:S(2)}) collective-permute-start(f32[2,64,32]{1,2,0:T(8,128)S(1)} %collective-permute-done.11), channel_id=1, source_target_pairs={{0,15},{1,0},{2,1},{3,2},{4,3},{5,4},{6,5},{7,6},{8,7},{9,8},{10,9... | collective-permute-start | bytes 49160 | tf_op jit(solution)/shard_map/ppermute | solution.py:35
  145.8 3.7 %collective-permute-start.12 = (f32[2,64,32]{1,2,0:T(8,128)S(1)}, f32[2,64,32]{1,2,0:T(8,128)S(1)}, u32[]{:S(2)}, u32[]{:S(2)}) collective-permute-start(f32[2,64,32]{1,2,0:T(8,128)S(1)} %collective-permute-done.10), channel_id=1, source_target_pairs={{0,1},{1,2},{2,3},{3,4},{4,5},{5,6},{6,7},{7,8},{8,9},{9,10},{10,1... | collective-permute-start | bytes 49160 | tf_op jit(solution)/shard_map/ppermute | solution.py:28
  149.4 4.6 %collective-permute-start.14 = (f32[2,64,32]{1,2,0:T(8,128)S(1)}, f32[2,64,32]{1,2,0:T(8,128)S(1)}, u32[]{:S(2)}, u32[]{:S(2)}) collective-permute-start(f32[2,64,32]{1,2,0:T(8,128)S(1)} %collective-permute-done.12), channel_id=1, source_target_pairs={{0,1},{1,2},{2,3},{3,4},{4,5},{5,6},{6,7},{7,8},{8,9},{9,10},{10,1... | collective-permute-start | bytes 49160 | tf_op jit(solution)/shard_map/ppermute | solution.py:28
Sparse Core Ops, SparseCore 0:
  40.1 40.0 all-gather.2
